TPU v7x, 32 devices: a whole 2x2x4 slice. The times are simulated.
32 devices in a mesh: dp: 8 (over z, x), mp: 4 (over y, core).
Axes of the slice: x: 2, y: 2, z: 4, core: 2. Of those that a mesh axis runs over, the one named last changes fastest.
Arguments:
- queries: bfloat16 [16, 16, 5120], P('dp', None, 'mp')
- key_value_cache: bfloat16 [128, 2, 128, 1024], P('dp', None, None, 'mp'), may hold values from -6 to 6
- slot_tags: int32 [128], P('dp'), may hold values from 0 to 15, as said below
- span_key_value: bfloat16 [16, 2, 16, 1024], P('dp', None, None, 'mp'), may hold values from -6 to 6
- answer_id: int32 [16], P('dp'), may hold values from 0 to 127
- w_cand: bfloat16 [5120, 128], P('mp')
Outputs:
- attended: bfloat16 [16, 16, 5120], P('dp', None, 'mp')
- chain_score: float32 [16], P('dp')
- answer_tally: float32 [1, 128], P(None, 'dp')
Inputs may be any that keep to these rules, and one draw needn't show every extreme that they name: `slot_tags`: among the 16 blocks of any one index of dp, at most 2 belong to the chains o * 2 to o * 2 + 1 of any one o, and for some o every index of dp holds exactly 2 such blocks. A chain may have no cached block.
All inputs are finite; a program needn't handle non-finite values.
Results may differ from a plain program's by a relative error of at most 0.0075.
Values may be sent and summed in bfloat16 or wider, within the bound.
No kernel may reach another device: no remote copies, remote signals or barrier semaphores. Data moves between devices by JAX's collectives and lax.ppermute only.
A program may use at most 128 MiB of HBM per device.

v0:
```python
import jax
import jax.numpy as jnp
from jax import lax
from jax.sharding import PartitionSpec as P

QUERY_HEADS = 40
KEY_VALUE_HEADS = 8
HEAD_SIZE = 128
NCAND = 128
PEER = 2
SAMPLES = 16
big_neg = -1e30


def block_terms(picked, blocks, causal):
    count = picked.shape[0]
    span = picked.shape[1]
    width = blocks.shape[2]
    heads_kv = blocks.shape[3] // HEAD_SIZE
    head_group = QUERY_HEADS // KEY_VALUE_HEADS
    query_rows = picked.reshape(count, span, heads_kv, head_group, HEAD_SIZE)
    lookup_matrix = blocks[:, 0].reshape(count, width, heads_kv, HEAD_SIZE)
    value_rows = blocks[:, 1].reshape(count, width, heads_kv, HEAD_SIZE)
    logit_rows = jnp.einsum(
        "nakgd,nbkd->nkgab", query_rows, lookup_matrix, preferred_element_type=jnp.float32
    ) * HEAD_SIZE ** (-0.5)
    if causal:
        allowed = jnp.arange(span)[:, None] >= jnp.arange(width)[None, :]
        logit_rows = jnp.where(allowed, logit_rows, big_neg)
    peaks = jnp.max(logit_rows, axis=-1)
    weights = jnp.exp(logit_rows - peaks[..., None])
    totals = jnp.sum(weights, axis=-1)
    summed_scores = jnp.einsum(
        "nkgab,nbkd->nkgad",
        weights.astype(jnp.bfloat16),
        value_rows,
        preferred_element_type=jnp.float32,
    )
    return (peaks, totals, summed_scores)


def merge_items(peaks, totals, summed_scores, member):
    member_f = member.astype(jnp.float32)
    masked = jnp.where(member[:, :, None, None, None], peaks[:, None], big_neg)
    chain_peak = jnp.max(masked, axis=0)
    item_peak = jnp.einsum("nc,ckga->nkga", member_f, chain_peak, precision=lax.Precision.HIGHEST)
    present = jnp.any(member, axis=1)
    factor = jnp.where(present[:, None, None, None], jnp.exp(peaks - item_peak), 0.0)
    chain_total = jnp.einsum(
        "nc,nkga->ckga", member_f, totals * factor, precision=lax.Precision.HIGHEST
    )
    chain_sum = jnp.einsum(
        "nc,nkgad->ckgad",
        member_f,
        summed_scores * factor[..., None],
        precision=lax.Precision.HIGHEST,
    )
    return (chain_peak, chain_total, chain_sum)


def fold_pair(first, second):
    overall = jnp.maximum(first[0], second[0])
    left = jnp.exp(first[0] - overall)
    right = jnp.exp(second[0] - overall)
    total = first[1] * left + second[1] * right
    summed_scores = first[2] * left[..., None] + second[2] * right[..., None]
    return (overall, total, summed_scores)


def per_device(queries, key_value_cache, slot_tags, span_key_value, answer_id, w_cand):
    accelerator_roster = lax.axis_size("dp")
    position = lax.axis_index("dp")
    chains_here = queries.shape[0]
    features = queries.shape[2]
    slots_here = slot_tags.shape[0]
    owner_index = slot_tags // chains_here
    chain_local = slot_tags % chains_here
    owner_hot = (
        owner_index[:, None] == jnp.arange(accelerator_roster, dtype=jnp.int32)[None, :]
    ).astype(jnp.int32)
    running = jnp.cumsum(owner_hot, axis=0) - 1
    rank_in = jnp.sum(owner_hot * running, axis=1)
    target = owner_index * PEER + rank_in
    places_all = accelerator_roster * PEER
    hit = (target[:, None] == jnp.arange(places_all, dtype=jnp.int32)[None, :]).astype(jnp.int32)
    source_row = jnp.sum(hit * jnp.arange(slots_here, dtype=jnp.int32)[:, None], axis=0)
    is_filled = jnp.sum(hit, axis=0) > 0
    send_chain = jnp.where(is_filled, jnp.sum(hit * chain_local[:, None], axis=0), chains_here)
    send_blocks = key_value_cache[source_row].reshape(
        (accelerator_roster, PEER) + key_value_cache.shape[1:]
    )
    send_chain = send_chain.reshape(accelerator_roster, PEER)
    blocks = lax.all_to_all(send_blocks, "dp", split_axis=0, concat_axis=0, tiled=True)
    places = lax.all_to_all(send_chain, "dp", split_axis=0, concat_axis=0, tiled=True)
    count = places.shape[0] * places.shape[1]
    flat_places = places.reshape(count)
    picked = queries[jnp.clip(flat_places, 0, chains_here - 1)]
    peaks, totals, summed_scores = block_terms(
        picked, blocks.reshape((count,) + blocks.shape[2:]), False
    )
    lead = places.shape
    peaks, totals, summed_scores, places = (
        peaks.reshape(lead + peaks.shape[1:]),
        totals.reshape(lead + totals.shape[1:]),
        summed_scores.reshape(lead + summed_scores.shape[1:]),
        places,
    )
    count = places.shape[0] * places.shape[1]
    member = places.reshape(count)[:, None] == jnp.arange(chains_here, dtype=jnp.int32)[None, :]
    remote = merge_items(
        peaks.reshape((count,) + peaks.shape[2:]),
        totals.reshape((count,) + totals.shape[2:]),
        summed_scores.reshape((count,) + summed_scores.shape[2:]),
        member,
    )
    own_span = block_terms(queries, span_key_value, True)
    final_peak, final_total, final_sum = fold_pair(own_span, remote)
    output = final_sum / final_total[..., None]
    output = jnp.transpose(output, (0, 3, 1, 2, 4)).reshape(chains_here, queries.shape[1], features)
    attended = output.astype(jnp.bfloat16)
    span = queries.shape[1]
    partial_logits = jnp.dot(
        attended.reshape(chains_here * span, features), w_cand, preferred_element_type=jnp.float32
    )
    logit_rows = lax.psum(partial_logits, "mp").reshape(chains_here, span, NCAND)
    top_logit = jnp.max(logit_rows, axis=-1, keepdims=True)
    log_norm = top_logit[..., 0] + jnp.log(jnp.sum(jnp.exp(logit_rows - top_logit), axis=-1))
    answer_hot = (answer_id[:, None] == jnp.arange(NCAND, dtype=jnp.int32)[None, :]).astype(
        jnp.float32
    )
    chosen_logit = jnp.sum(logit_rows * answer_hot[:, None, :], axis=-1)
    chain_score = jnp.mean(chosen_logit - log_norm, axis=-1)
    prompt_count = accelerator_roster * chains_here // SAMPLES
    global_chain = position * chains_here + jnp.arange(chains_here, dtype=jnp.int32)
    prompt_hot = (
        (global_chain // SAMPLES)[:, None] == jnp.arange(prompt_count, dtype=jnp.int32)[None, :]
    ).astype(jnp.float32)
    tally_terms = jnp.dot(
        prompt_hot.T, chain_score[:, None] * answer_hot, precision=lax.Precision.HIGHEST
    )
    answer_tally = lax.psum_scatter(tally_terms, "dp", scatter_dimension=1, tiled=True)
    return (attended, chain_score, answer_tally)


def solution(mesh):
    in_specs = (
        P("dp", None, "mp"),
        P("dp", None, None, "mp"),
        P("dp"),
        P("dp", None, None, "mp"),
        P("dp"),
        P("mp", None),
    )
    out_specs = (P("dp", None, "mp"), P("dp"), P(None, "dp"))
    return jax.shard_map(
        per_device, mesh=mesh, in_specs=in_specs, out_specs=out_specs, check_vma=False
    )
```

profile of v0, /device:TPU:0, one launch (start us, length us, event | category | flops | bytes accessed | tf_op | source)
XLA Modules:
  0.0 165.2 jit_solution(9929074711548436345)
XLA Ops:
  7.2 0.8 and_select_fusion.1
  8.1 0.2 select_reduce_fusion.3
  8.4 0.7 select_n.71
  9.1 7.3 %all-to-all-start = ((s32[8,1,2]{2,1,0:T(1,128)}), s32[8,1,2]{2,1,0:T(1,128)S(1)}, u32[]{:S(2)}, u32[]{:S(2)}) async-start(s32[8,1,2]{2,1,0:T(1,128)} %bitcast.5), calls=%async_computation | async-start | bytes 8192 | tf_op jit(solution)/shard_map/all_to_all | solution.py:94
  16.4 2.0 %gather_fusion = bf16[16,2,128,256]{3,2,1,0:T(8,128)(2,1)} fusion(bf16[16,2,128,256]{3,2,1,0:T(8,128)(2,1)S(1)} %copy-done, s32[1024]{0:T(1024)S(1)} %pad_clamp_fusion.1), kind=kCustom, calls=%fused_computation | custom fusion | bytes 4194368 | tf_op jit(solution)/shard_map/gather | solution.py:89
  18.4 3.9 %copy.89 = bf16[8,2,2,128,256]{3,4,1,2,0:T(8,128)(2,1)} copy(bf16[8,2,2,128,256]{4,3,2,1,0:T(8,128)(2,1)} %bitcast.89) | data formatting | bytes 4194304 | tf_op jit(solution)/shard_map/reshape | solution.py:89
  22.3 0.5 all-to-all-done
  22.8 5.7 %all-to-all-start.1 = ((bf16[8,2,2,128,256]{3,4,1,2,0:T(8,128)(2,1)}), bf16[8,2,2,128,256]{3,4,1,2,0:T(8,128)(2,1)}, u32[]{:S(2)}, u32[]{:S(2)}) async-start(bf16[8,2,2,128,256]{3,4,1,2,0:T(8,128)(2,1)} %copy.89), calls=%async_computation.1 | async-start | bytes 4194304 | tf_op jit(solution)/shard_map/all_to_all | solution.py:93
  28.7 0.3 fusion.64
  29.1 0.5 broadcast.247
  29.6 0.7 fusion.60
  30.4 1.4 gather_fusion.1
  31.8 1.8 %reshape.177 = bf16[16,16,2,5,128]{4,3,2,1,0:T(8,128)(2,1)S(1)} reshape(bf16[16,16,1280]{2,1,0:T(8,128)(2,1)} %gather_fusion.1) | data formatting | bytes 1310720 | tf_op jit(solution)/shard_map/reshape | solution.py:21
  33.7 42.5 %all-to-all-done.1 = bf16[8,2,2,128,256]{3,4,1,2,0:T(8,128)(2,1)} async-done(((bf16[8,2,2,128,256]{3,4,1,2,0:T(8,128)(2,1)}), bf16[8,2,2,128,256]{3,4,1,2,0:T(8,128)(2,1)}, u32[]{:S(2)}, u32[]{:S(2)}) %all-to-all-start.1) | async-done | bytes 2097184 | tf_op jit(solution)/shard_map/all_to_all | solution.py:93
  76.2 1.7 %copy.90 = bf16[8,2,2,128,256]{3,4,1,0,2:T(8,128)(2,1)S(1)} copy(bf16[8,2,2,128,256]{3,4,1,2,0:T(8,128)(2,1)} %all-to-all-done.1) | data formatting | bytes 4194304 | tf_op jit(solution)/shard_map/all_to_all | solution.py:93
  78.0 0.2 fusion.61
  78.2 0.6 fusion.63
  78.9 0.2 fusion.12
  79.2 0.8 fusion.3
  80.0 1.4 convolution_multiply_fusion
  81.5 1.3 fusion.1
  82.8 0.2 fusion.14
  83.0 0.3 fusion.10
  83.4 0.2 fusion.65
  83.6 10.1 %psum.7 = f32[32,128]{1,0:T(8,128)S(1)} all-reduce(f32[32,128]{1,0:T(8,128)S(1)} %fusion.65), channel_id=1, replica_groups=mesh['dp'=8,'mp'=4] {'mp'}, use_global_device_ids=true, to_apply=%region_11.12 | all-reduce | flops 4096 | bytes 32768 | tf_op jit(solution)/shard_map/psum | solution.py:125
  93.7 0.1 reduce_max.45
  93.8 0.2 exponential_reduce_fusion
  94.1 0.1 reduce_sum.95
  94.3 1.0 convolution_bitcast_fusion.1
  95.2 0.7 convert_element_type.36
  96.0 61.1 %reduce-scatter.4.cloned.1.call-done = f32[16,1]{1,0:T(8,128)} async-done(((f32[128,1]{1,0:T(8,128)}), f32[16,1]{1,0:T(8,128)}) %reduce-scatter.4.cloned.1.call-update) | async-done | bytes 80
  157.1 1.3 copy.124
  (45 shorter events, 1.2 us)
Async XLA Ops:
  7.2 9.2 %copy-start = (bf16[16,2,128,256]{3,2,1,0:T(8,128)(2,1)S(1)}, bf16[16,2,128,256]{3,2,1,0:T(8,128)(2,1)}, u32[]{:S(2)}) copy-start(bf16[16,2,128,256]{3,2,1,0:T(8,128)(2,1)} %param.7) | copy-start | bytes 6291460
  9.1 13.7 %all-to-all-start = ((s32[8,1,2]{2,1,0:T(1,128)}), s32[8,1,2]{2,1,0:T(1,128)S(1)}, u32[]{:S(2)}, u32[]{:S(2)}) async-start(s32[8,1,2]{2,1,0:T(1,128)} %bitcast.5), calls=%async_computation | async-start | bytes 8192 | tf_op jit(solution)/shard_map/all_to_all | solution.py:94
  22.3 6.2 %copy-start.1 = (bf16[2,16,1280]{2,1,0:T(8,128)(2,1)S(1)}, bf16[2,16,1280]{2,1,0:T(8,128)(2,1)}, u32[]{:S(2)}) copy-start(bf16[2,16,1280]{2,1,0:T(8,128)(2,1)} %param.6) | copy-start | bytes 245764
  22.3 6.3 %copy-start.3 = (bf16[2,2,16,256]{3,2,1,0:T(8,128)(2,1)S(1)}, bf16[2,2,16,256]{3,2,1,0:T(8,128)(2,1)}, u32[]{:S(2)}) copy-start(bf16[2,2,16,256]{3,2,1,0:T(8,128)(2,1)} %param.9) | copy-start | bytes 98308
  22.3 6.8 %copy-start.4 = (s32[2]{0:T(128)S(1)}, s32[2]{0:T(128)}, u32[]{:S(2)}) copy-start(s32[2]{0:T(128)} %param.10) | copy-start | bytes 28
  22.8 53.4 %all-to-all-start.1 = ((bf16[8,2,2,128,256]{3,4,1,2,0:T(8,128)(2,1)}), bf16[8,2,2,128,256]{3,4,1,2,0:T(8,128)(2,1)}, u32[]{:S(2)}, u32[]{:S(2)}) async-start(bf16[8,2,2,128,256]{3,4,1,2,0:T(8,128)(2,1)} %copy.89), calls=%async_computation.1 | async-start | bytes 4194304 | tf_op jit(solution)/shard_map/all_to_all | solution.py:93
  28.4 128.6 %reduce-scatter.4.cloned.1.call-start = ((), (), s32[]{:S(2)}) async-start(), calls=%async_computation.3 | async-start | bytes 73728
  81.5 1.9 %copy-start.2 = (bf16[1280,128]{1,0:T(8,128)(2,1)S(1)}, bf16[1280,128]{1,0:T(8,128)(2,1)}, u32[]{:S(2)}) copy-start(bf16[1280,128]{1,0:T(8,128)(2,1)} %param.11) | copy-start | bytes 983044
  94.2 64.1 %copy-start.5 = (f32[2]{0:T(128)}, f32[2]{0:T(128)S(1)}, u32[]{:S(2)}) copy-start(f32[2]{0:T(128)S(1)} %broadcast_multiply_fusion) | copy-start | bytes 28
Sparse Core Ops, SparseCore 0:
  95.4 61.6 reduce-scatter.3
where the time goes:
time: 166 us; the launch traced here: 165 us
  waiting for transfers between devices  104 us (63%)
  local copies, waits for them, and re-layouts  14.9 us (9%)
  between operations  14.3 us (9%)
  starting transfers between devices  13 us (8%)
  blocking collectives  10.1 us (6%)
  matrix products  5.37 us (3%)
  other arithmetic  3.42 us (2%)
    unnamed x2, waiting for transfers between devices  61.1 us
    all_to_all x1, waiting for transfers between devices, per_device(): lax.all_to_all(send_blocks, 'dp', split_axis=0, concat_axis=0, tiled=True)  42.5 us
    psum x1, blocking collectives, per_device(): lax.psum(partial_logits, 'mp').reshape(chains_here, span, NCAND)  10.1 us
    all_to_all x1, starting transfers between devices, per_device(): lax.all_to_all(send_chain, 'dp', split_axis=0, concat_axis=0, tiled=True)  7.28 us
    all_to_all x1, starting transfers between devices, per_device(): lax.all_to_all(send_blocks, 'dp', split_axis=0, concat_axis=0, tiled=True)  5.66 us
    reshape x1, local copies, waits for them, and re-layouts, per_device(): key_value_cache[source_row]  3.92 us
  transfers between devices with their start and end apart: 3, of which 3 were waited for; matrix products, arithmetic and copies ran while one was open for 7% of the time, Pallas kernels for 0%

commit v1 on v0

--- a/solution.py
+++ b/solution.py
@@ -10,6 +10,25 @@
 PEER = 2
 SAMPLES = 16
 big_neg = -1e30
+
+
+def fit_page(z, which_dim, s0):
+    o_now = z.shape
+    t_next = jnp.moveaxis(
+        z.reshape(*o_now[:which_dim], s0, o_now[which_dim] // s0, *o_now[which_dim + 1 :]),
+        which_dim,
+        0,
+    )
+    return t_next
+
+
+def push_tails_on_mesh(mine, axis_k):
+    mine = jnp.moveaxis(mine, 0, axis_k)
+    block_next = mine.shape
+    reply = mine.reshape(
+        *block_next[:axis_k], block_next[axis_k] * block_next[axis_k + 1], *block_next[axis_k + 2 :]
+    )
+    return reply
 
 
 def block_terms(picked, blocks, causal):
@@ -90,7 +109,18 @@
         (accelerator_roster, PEER) + key_value_cache.shape[1:]
     )
     send_chain = send_chain.reshape(accelerator_roster, PEER)
-    blocks = lax.all_to_all(send_blocks, "dp", split_axis=0, concat_axis=0, tiled=True)
+    spare, n_now = (lax.axis_size("dp"), lax.axis_index("dp"))
+    work_now = fit_page(send_blocks, 0, spare)
+    stack_in = [work_now[n_now]]
+    it = 1
+    while it < spare:
+        value_now = work_now[n_now ^ it]
+        stack_in.append(
+            lax.ppermute(value_now, axis_name="dp", perm=[(p, p ^ it) for p in range(spare)])
+        )
+        it += 1
+    work_now = jnp.stack(stack_in, axis=0)[n_now ^ jnp.arange(spare)]
+    blocks = push_tails_on_mesh(work_now, 0)
     places = lax.all_to_all(send_chain, "dp", split_axis=0, concat_axis=0, tiled=True)
     count = places.shape[0] * places.shape[1]
     flat_places = places.reshape(count)

time: 166 us -> 183 us (1.10)
  local copies, waits for them, and re-layouts: 14.9 us -> 35.9 us
  waiting for transfers between devices: 104 us -> 88.7 us
  starting transfers between devices: 13 us -> 19.1 us
  other arithmetic: 3.42 us -> 6.28 us
  matrix products: 5.37 us -> 7.76 us
    all_to_all x1 -> x0, waiting for transfers between devices: 42.5 us -> none  [per_device(): lax.all_to_all(send_blocks, 'dp', split_axis=0, concat_axis=0, tiled=True)]
    ppermute x0 -> x7, waiting for transfers between devices: none -> 20.3 us  [per_device(): lax.ppermute(value_now, axis_name='dp', perm=[(p, p ^ it) for p in range(...]
    unnamed x13 -> x45, local copies, waits for them, and re-layouts: 1.31 us -> 14.7 us
    ppermute x0 -> x7, starting transfers between devices: none -> 11.8 us  [per_device(): lax.ppermute(value_now, axis_name='dp', perm=[(p, p ^ it) for p in range(...]
    unnamed x2, waiting for transfers between devices: 61.1 us -> 67.3 us
    all_to_all x1 -> x0, starting transfers between devices: 5.66 us -> none  [per_device(): lax.all_to_all(send_blocks, 'dp', split_axis=0, concat_axis=0, tiled=True)]
    reshape x1 -> x0, local copies, waits for them, and re-layouts: 3.92 us -> none  [per_device(): key_value_cache[source_row]]
    gather x0 -> x1, local copies, waits for them, and re-layouts: none -> 3.56 us  [per_device(): work_now = jnp.stack(stack_in, axis=0)[n_now ^ jnp.arange(spare)]]
  transfers between devices with their start and end apart: 3 -> 9, of which waited for: 3 -> 4; matrix products, arithmetic and copies ran while one was open for 7% -> 10% of each run, Pallas kernels for 0% -> 0%
where the time goes in v1:
time: 183 us; the launch traced here: 182 us
  waiting for transfers between devices  88.7 us (48%)
  local copies, waits for them, and re-layouts  35.9 us (20%)
  starting transfers between devices  19.1 us (10%)
  between operations  14.4 us (8%)
  blocking collectives  10.1 us (6%)
  matrix products  7.76 us (4%)
  other arithmetic  6.28 us (3%)
    unnamed x2, waiting for transfers between devices  67.3 us
    ppermute x7, waiting for transfers between devices, per_device(): lax.ppermute(value_now, axis_name='dp', perm=[(p, p ^ it) for p in range(...  20.3 us
    unnamed x45, local copies, waits for them, and re-layouts  14.7 us
    ppermute x7, starting transfers between devices, per_device(): lax.ppermute(value_now, axis_name='dp', perm=[(p, p ^ it) for p in range(...  11.8 us
    psum x1, blocking collectives, per_device(): lax.psum(partial_logits, 'mp').reshape(chains_here, span, NCAND)  10.1 us
    all_to_all x1, starting transfers between devices, per_device(): lax.all_to_all(send_chain, 'dp', split_axis=0, concat_axis=0, tiled=True)  7.28 us
  transfers between devices with their start and end apart: 9, of which 4 were waited for; matrix products, arithmetic and copies ran while one was open for 10% of the time, Pallas kernels for 0%

profile of v1, /device:TPU:0, one launch (start us, length us, event | category | flops | bytes accessed | tf_op | source)
XLA Modules:
  0.0 182.3 jit_solution(14513685660029986573)
XLA Ops:
  9.1 7.3 %all-to-all-start = ((s32[8,1,2]{2,1,0:T(1,128)}), s32[8,1,2]{2,1,0:T(1,128)S(1)}, u32[]{:S(2)}, u32[]{:S(2)}) async-start(s32[8,1,2]{2,1,0:T(1,128)} %bitcast.5), calls=%async_computation | async-start | bytes 8192 | tf_op jit(solution)/shard_map/all_to_all | solution.py:124
  17.2 1.0 reshape.184
  18.9 1.3 fusion.35
  21.8 1.1 all-to-all-done
  24.1 2.0 %gather_fusion = bf16[16,2,128,256]{3,2,1,0:T(8,128)(2,1)} fusion(bf16[16,2,128,256]{3,2,1,0:T(8,128)(2,1)S(1)} %copy-done, s32[1024]{0:T(1024)S(1)} %pad_clamp_fusion.2), kind=kCustom, calls=%fused_computation | custom fusion | bytes 4194368 | tf_op jit(solution)/shard_map/gather | solution.py:108
  26.1 2.7 %dynamic-slice_bitcast_fusion = (bf16[1,2,2,128,256]{4,3,2,1,0:T(8,128)(2,1)S(1)}, bf16[1,2,2,128,256]{4,3,2,1,0:T(8,128)(2,1)S(1)}, bf16[1,2,2,128,256]{4,3,2,1...) fusion(bf16[8,1,2,2,128,256]{5,4,3,2,0,1:T(8,128)(2,1)} %bitcas, ...), kind=kLoop, calls=%fused_computation.35 | loop fusion | bytes 4194336 | tf_op jit(solution)/shard_map/squeeze | solution.py:117
  29.7 1.5 collective-permute-start.1
  31.2 1.1 collective-permute-start.2
  32.3 1.8 collective-permute-start.3
  34.1 1.5 collective-permute-start.4
  35.6 1.0 iota_compare_fusion.5
  37.3 1.7 reshape.185
  39.0 3.3 %collective-permute-start.5 = (bf16[1,2,2,128,256]{4,3,2,1,0:T(8,128)(2,1)S(1)}, bf16[1,2,2,128,256]{4,3,2,1,0:T(8,128)(2,1)S(1)}, u32[]{:S(2)}, u32[]{:S(2)}) collective-permute-start(bf16[1,2,2,128,256]{4,3,2,1,0:T(8,128)(2,1)S(1)} %get-tuple-element.13), channel_id=1, source_target_pairs={{0,24},{4,28},{8,16},{12,20},{16,8},{20,12},{24,0},{28,4},{1,25},{... | collective-permute-start | bytes 786440 | tf_op jit(solution)/shard_map/ppermute | solution.py:119
  42.3 1.7 bitcast_dynamic-update-slice_fusion.6
  43.9 4.7 %collective-permute-done.1 = bf16[1,2,2,128,256]{4,3,2,1,0:T(8,128)(2,1)} collective-permute-done((bf16[1,2,2,128,256]{4,3,2,1,0:T(8,128)(2,1)}, bf16[1,2,2,128,256]{4,3,2,1,0:T(8,128)(2,1)}, u32[]{:S(2)}, u32[]{:S(2)}) %collective-permute-start.1) | collective-permute-done | bytes 262176 | tf_op jit(solution)/shard_map/ppermute | solution.py:119
  48.7 1.8 %collective-permute-start.6 = (bf16[1,2,2,128,256]{4,3,2,1,0:T(8,128)(2,1)S(1)}, bf16[1,2,2,128,256]{4,3,2,1,0:T(8,128)(2,1)S(1)}, u32[]{:S(2)}, u32[]{:S(2)}) collective-permute-start(bf16[1,2,2,128,256]{4,3,2,1,0:T(8,128)(2,1)S(1)} %get-tuple-element.12), channel_id=1, source_target_pairs={{0,28},{4,24},{8,20},{12,16},{16,12},{20,8},{24,4},{28,0},{1,29},{... | collective-permute-start | bytes 786440 | tf_op jit(solution)/shard_map/ppermute | solution.py:119
  50.5 1.7 bitcast_dynamic-update-slice_fusion.5
  52.2 1.7 bitcast_dynamic-update-slice_fusion.4
  53.9 1.7 bitcast_dynamic-update-slice_fusion.3
  55.5 15.6 %collective-permute-done.4 = bf16[1,2,2,128,256]{4,3,2,1,0:T(8,128)(2,1)} collective-permute-done((bf16[1,2,2,128,256]{4,3,2,1,0:T(8,128)(2,1)}, bf16[1,2,2,128,256]{4,3,2,1,0:T(8,128)(2,1)}, u32[]{:S(2)}, u32[]{:S(2)}) %collective-permute-start.4) | collective-permute-done | bytes 262176 | tf_op jit(solution)/shard_map/ppermute | solution.py:119
  71.1 1.7 bitcast_dynamic-update-slice_fusion.2
  74.3 3.6 %gather_fusion.1 = bf16[8,2,2,128,256]{4,3,2,1,0:T(8,128)(2,1)} fusion(bf16[8,2,2,128,256]{4,3,2,1,0:T(8,128)(2,1)} %bitcast.122, s32[1024]{0:T(1024)S(1)} %pad_clamp_fusion.1), kind=kCustom, calls=%fused_computation.1 | custom fusion | bytes 4194336 | tf_op jit(solution)/shard_map/gather | solution.py:122
  77.8 2.7 %fusion.61 = (bf16[16,1,128,256]{3,2,1,0:T(8,128)(2,1)S(1)}, bf16[16,1,128,256]{3,2,1,0:T(8,128)(2,1)}) fusion(bf16[16,2,128,256]{3,2,1,0:T(8,128)(2,1)} %bitcast.120), kind=kLoop, calls=%fused_computation.123 | loop fusion | bytes 4194304 | tf_op jit(solution)/shard_map/slice | solution.py:41
  80.5 1.3 copy.143
  81.9 2.1 %fusion.63 = (f32[16,2,5,16]{3,2,1,0:T(8,128)S(1)}, f32[16,2,5,16,128]{4,3,2,1,0:T(8,128)S(1)}) fusion(bf16[16,128,2,128,1]{1,3,4,2,0:T(8,128)(2,1)} %bitcast.121, bf16[16,16,2,5,128]{4,3,2,1,0:T(8,128)(2,1)} %reshape.185), kind=kOutput, calls=%fused_computation.125 | convolution fusion | flops 84538880 | bytes 3024896 | tf_op jit(solution)/shard_map/nakgd,nbkd->nkgab/dot_general | solution.py:43
  87.9 2.3 %copy.144 = bf16[16,1,128,256]{2,3,0,1:T(8,128)(2,1)} copy(bf16[16,1,128,256]{3,2,1,0:T(8,128)(2,1)} %get-tuple-element.11) | data formatting | bytes 2097152
  90.3 2.3 %convolution_multiply_fusion = f32[16,2,5,16,128]{4,3,2,1,0:T(8,128)S(1)} fusion(bf16[16,128,2,128,1]{1,3,4,2,0:T(8,128)(2,1)} %bitcast.123, f32[16,2,5,16,128]{4,3,2,1,0:T(8,128)S(1)} %get-tuple-element.29, f32[16,2,5,16]{3,2,1,0:T(8,128)} %copy.117, f32[16,2,5,16]{3,2,1,0:T(8,128)S(1)} %get-tuple-element.28), kind=kOutput, calls=%fused_computation.3 | convolution fusion | flops 84869120 | bytes 3690496 | tf_op jit(solution)/shard_map/nkgab,nbkd->nkgad/dot_general | solution.py:52
  92.6 1.3 fusion.1
  94.5 10.1 %psum.7 = f32[32,128]{1,0:T(8,128)S(1)} all-reduce(f32[32,128]{1,0:T(8,128)S(1)} %fusion.66), channel_id=1, replica_groups=mesh['dp'=8,'mp'=4] {'mp'}, use_global_device_ids=true, to_apply=%region_11.12 | all-reduce | flops 4096 | bytes 32768 | tf_op jit(solution)/shard_map/psum | solution.py:155
  105.2 1.0 convolution_bitcast_fusion.1
  106.9 67.3 %reduce-scatter.4.cloned.1.call-done = f32[16,1]{1,0:T(8,128)} async-done(((f32[128,1]{1,0:T(8,128)}), f32[16,1]{1,0:T(8,128)}) %reduce-scatter.4.cloned.1.call-update) | async-done | bytes 80
  174.2 1.3 copy.142
  (91 shorter events, 15.0 us)
Async XLA Ops:
  7.2 17.0 %copy-start = (bf16[16,2,128,256]{3,2,1,0:T(8,128)(2,1)S(1)}, bf16[16,2,128,256]{3,2,1,0:T(8,128)(2,1)}, u32[]{:S(2)}) copy-start(bf16[16,2,128,256]{3,2,1,0:T(8,128)(2,1)} %param.7) | copy-start | bytes 6291460
  9.1 13.8 %all-to-all-start = ((s32[8,1,2]{2,1,0:T(1,128)}), s32[8,1,2]{2,1,0:T(1,128)S(1)}, u32[]{:S(2)}, u32[]{:S(2)}) async-start(s32[8,1,2]{2,1,0:T(1,128)} %bitcast.5), calls=%async_computation | async-start | bytes 8192 | tf_op jit(solution)/shard_map/all_to_all | solution.py:124
  16.4 157.9 %reduce-scatter.4.cloned.1.call-start = ((), (), s32[]{:S(2)}) async-start(), calls=%async_computation.2 | async-start | bytes 73728
  20.5 0.7 copy-start.2
  26.1 10.6 %copy-start.1 = (bf16[2,16,1280]{2,1,0:T(8,128)(2,1)S(1)}, bf16[2,16,1280]{2,1,0:T(8,128)(2,1)}, u32[]{:S(2)}) copy-start(bf16[2,16,1280]{2,1,0:T(8,128)(2,1)} %param.6) | copy-start | bytes 245764
  28.8 10.2 %collective-permute-start = (bf16[1,2,2,128,256]{4,3,2,1,0:T(8,128)(2,1)}, bf16[1,2,2,128,256]{4,3,2,1,0:T(8,128)(2,1)}, u32[]{:S(2)}, u32[]{:S(2)}) collective-permute-start(bf16[1,2,2,128,256]{4,3,2,1,0:T(8,128)(2,1)} %get-tuple-element.18), channel_id=1, source_target_pairs={{0,4},{4,0},{8,12},{12,8},{16,20},{20,16},{24,28},{28,24},{1,5},{5... | collective-permute-start | bytes 786440 | tf_op jit(solution)/shard_map/ppermute | solution.py:119
  29.7 18.9 %collective-permute-start.1 = (bf16[1,2,2,128,256]{4,3,2,1,0:T(8,128)(2,1)}, bf16[1,2,2,128,256]{4,3,2,1,0:T(8,128)(2,1)}, u32[]{:S(2)}, u32[]{:S(2)}) collective-permute-start(bf16[1,2,2,128,256]{4,3,2,1,0:T(8,128)(2,1)} %get-tuple-element.17), channel_id=1, source_target_pairs={{0,8},{4,12},{8,0},{12,4},{16,24},{20,28},{24,16},{28,20},{1,9},{5... | collective-permute-start | bytes 786440 | tf_op jit(solution)/shard_map/ppermute | solution.py:119
  31.2 21.0 %collective-permute-start.2 = (bf16[1,2,2,128,256]{4,3,2,1,0:T(8,128)(2,1)}, bf16[1,2,2,128,256]{4,3,2,1,0:T(8,128)(2,1)}, u32[]{:S(2)}, u32[]{:S(2)}) collective-permute-start(bf16[1,2,2,128,256]{4,3,2,1,0:T(8,128)(2,1)} %get-tuple-element.16), channel_id=1, source_target_pairs={{0,12},{4,8},{8,4},{12,0},{16,28},{20,24},{24,20},{28,16},{1,13},{... | collective-permute-start | bytes 786440 | tf_op jit(solution)/shard_map/ppermute | solution.py:119
  32.3 21.5 %collective-permute-start.3 = (bf16[1,2,2,128,256]{4,3,2,1,0:T(8,128)(2,1)}, bf16[1,2,2,128,256]{4,3,2,1,0:T(8,128)(2,1)}, u32[]{:S(2)}, u32[]{:S(2)}) collective-permute-start(bf16[1,2,2,128,256]{4,3,2,1,0:T(8,128)(2,1)} %get-tuple-element.15), channel_id=1, source_target_pairs={{0,16},{4,20},{8,24},{12,28},{16,0},{20,4},{24,8},{28,12},{1,17},{... | collective-permute-start | bytes 786440 | tf_op jit(solution)/shard_map/ppermute | solution.py:119
  34.1 37.0 %collective-permute-start.4 = (bf16[1,2,2,128,256]{4,3,2,1,0:T(8,128)(2,1)}, bf16[1,2,2,128,256]{4,3,2,1,0:T(8,128)(2,1)}, u32[]{:S(2)}, u32[]{:S(2)}) collective-permute-start(bf16[1,2,2,128,256]{4,3,2,1,0:T(8,128)(2,1)} %get-tuple-element.14), channel_id=1, source_target_pairs={{0,20},{4,16},{8,28},{12,24},{16,4},{20,0},{24,12},{28,8},{1,21},{... | collective-permute-start | bytes 786440 | tf_op jit(solution)/shard_map/ppermute | solution.py:119
  35.6 18.2 %copy-start.10 = (s32[16]{0:T(128)}, s32[16]{0:T(128)S(1)}, u32[]{:S(2)}) copy-start(s32[16]{0:T(128)S(1)} %eq.74) | copy-start | bytes 196
  39.0 33.8 %collective-permute-start.5 = (bf16[1,2,2,128,256]{4,3,2,1,0:T(8,128)(2,1)S(1)}, bf16[1,2,2,128,256]{4,3,2,1,0:T(8,128)(2,1)S(1)}, u32[]{:S(2)}, u32[]{:S(2)}) collective-permute-start(bf16[1,2,2,128,256]{4,3,2,1,0:T(8,128)(2,1)S(1)} %get-tuple-element.13), channel_id=1, source_target_pairs={{0,24},{4,28},{8,16},{12,20},{16,8},{20,12},{24,0},{28,4},{1,25},{... | collective-permute-start | bytes 786440 | tf_op jit(solution)/shard_map/ppermute | solution.py:119
  48.7 24.9 %collective-permute-start.6 = (bf16[1,2,2,128,256]{4,3,2,1,0:T(8,128)(2,1)S(1)}, bf16[1,2,2,128,256]{4,3,2,1,0:T(8,128)(2,1)S(1)}, u32[]{:S(2)}, u32[]{:S(2)}) collective-permute-start(bf16[1,2,2,128,256]{4,3,2,1,0:T(8,128)(2,1)S(1)} %get-tuple-element.12), channel_id=1, source_target_pairs={{0,28},{4,24},{8,20},{12,16},{16,12},{20,8},{24,4},{28,0},{1,29},{... | collective-permute-start | bytes 786440 | tf_op jit(solution)/shard_map/ppermute | solution.py:119
  81.9 3.0 %copy-start.15 = (pred[16,2]{0,1:T(4,128)(4,1)S(1)}, pred[16,2]{0,1:T(4,128)(4,1)}, u32[]{:S(2)}) copy-start(pred[16,2]{0,1:T(4,128)(4,1)} %get-tuple-element.24) | copy-start | bytes 100
  81.9 3.1 %copy-start.11 = (s32[16]{0:T(128)S(1)}, s32[16]{0:T(128)}, u32[]{:S(2)}) copy-start(s32[16]{0:T(128)} %copy-done.10) | copy-start | bytes 196
  81.9 3.2 %copy-start.14 = (pred[16]{0:T(512)(128)(4,1)S(1)}, pred[16]{0:T(512)(128)(4,1)}, u32[]{:S(2)}) copy-start(pred[16]{0:T(512)(128)(4,1)} %get-tuple-element.25) | copy-start | bytes 52
  81.9 5.3 %copy-start.5 = (f32[2,2,5,16]{3,2,1,0:T(8,128)S(1)}, f32[2,2,5,16]{3,2,1,0:T(8,128)}, u32[]{:S(2)}) copy-start(f32[2,2,5,16]{3,2,1,0:T(8,128)} %fusion.18) | copy-start | bytes 3844
  90.2 2.3 %copy-start.12 = (s32[16]{0:T(128)S(1)}, s32[16]{0:T(128)}, u32[]{:S(2)}) copy-start(s32[16]{0:T(128)} %copy-done.10) | copy-start | bytes 196
  90.2 3.6 %copy-start.3 = (f32[2,2,5,16,16]{3,4,2,1,0:T(8,128)S(1)}, f32[2,2,5,16,16]{3,4,2,1,0:T(8,128)}, u32[]{:S(2)}) copy-start(f32[2,2,5,16,16]{3,4,2,1,0:T(8,128)} %copy-done.2) | copy-start | bytes 61444
  90.2 3.6 %copy-start.6 = (bf16[2,16,2,128]{3,2,1,0:T(2,128)(2,1)S(1)}, bf16[2,16,2,128]{3,2,1,0:T(2,128)(2,1)}, u32[]{:S(2)}) copy-start(bf16[2,16,2,128]{3,2,1,0:T(2,128)(2,1)} %reshape_squeeze.13) | copy-start | bytes 49156
  90.2 3.6 %copy-start.7 = (f32[2,16,2,5]{1,3,2,0:T(8,128)S(1)}, f32[2,16,2,5]{1,3,2,0:T(8,128)}, u32[]{:S(2)}) copy-start(f32[2,16,2,5]{1,3,2,0:T(8,128)} %copy.112) | copy-start | bytes 3844
  90.2 3.6 %copy-start.8 = (f32[2,16,2,5]{1,3,2,0:T(8,128)S(1)}, f32[2,16,2,5]{1,3,2,0:T(8,128)}, u32[]{:S(2)}) copy-start(f32[2,16,2,5]{1,3,2,0:T(8,128)} %copy.120) | copy-start | bytes 3844
  90.3 3.6 %copy-start.9 = (f32[2,16,2,5]{1,3,2,0:T(8,128)S(1)}, f32[2,16,2,5]{1,3,2,0:T(8,128)}, u32[]{:S(2)}) copy-start(f32[2,16,2,5]{1,3,2,0:T(8,128)} %copy.123) | copy-start | bytes 3844
  92.5 1.8 copy-start.4
  92.6 12.2 %copy-start.13 = (f32[2,128]{1,0:T(2,128)S(1)}, f32[2,128]{1,0:T(2,128)}, u32[]{:S(2)}) copy-start(f32[2,128]{1,0:T(2,128)} %fusion.35) | copy-start | bytes 3076
  92.6 12.6 %copy-start.16 = (s32[2]{0:T(128)S(1)}, s32[2]{0:T(128)}, u32[]{:S(2)}) copy-start(s32[2]{0:T(128)} %param.10) | copy-start | bytes 28
  105.2 70.3 %copy-start.17 = (f32[2]{0:T(128)}, f32[2]{0:T(128)S(1)}, u32[]{:S(2)}) copy-start(f32[2]{0:T(128)S(1)} %broadcast_multiply_fusion) | copy-start | bytes 28
Sparse Core Ops, SparseCore 0:
  106.3 67.8 reduce-scatter.3
